TPU v7x, 32 devices: a whole 2x2x4 slice. The times are simulated.
32 devices in a mesh: groups: 2 (over y), row: 4 (over z), col: 2 (over x), sub: 2 (over core).
Axes of the slice: x: 2, y: 2, z: 4, core: 2. Of those that a mesh axis runs over, the one named last changes fastest.
Arguments:
- matrix: float32 [16384, 8192], P(('groups', 'row'), ('col', 'sub')), parts along dimension 0, may hold values from -60 to 60
- basis_vectors: float32 [16384, 1024], P(('groups', 'row'), ('col', 'sub')), parts along dimension 0, may hold values from -0.0625 to 0.0625
- split_size: int32 [2], P('groups'), parts along dimension 0, may hold values from 256 to 767
Outputs:
- children: float32 [2, 2048, 1024], P('sub', ('groups', 'row'), 'col'), parts along dimension 1
There are 2 independent parts, one for each index of `groups`. A program takes and returns all parts, laid end to end along the dimension named above; each array names one. Nothing has to cross between parts.
Inputs may be any that keep to these rules, and one draw needn't show every extreme that they name: The second subspace has 1024 minus split_size vectors.
All inputs are finite; a program needn't handle non-finite values.
Results may differ from a plain program's by a relative error of at most 0.00011.
Values sent between devices are 32-bit elements; how exact they have to be, the bound alone decides.
A program may use at most 128 MiB of HBM per device.

v0:
```python
import jax
import jax.numpy as jnp
from jax import lax
from jax.sharding import PartitionSpec as P


def shards(matrix, basis_vectors, split_size):
    R = lax.axis_size("row")
    S = lax.axis_size("sub")
    C = lax.axis_size("col") * S
    m, kd = basis_vectors.shape
    K = kd * C
    n = matrix.shape[1]
    per = n // m
    piece = m // R
    spread = lax.all_to_all(basis_vectors, "row", split_axis=0, concat_axis=0, tiled=True)
    mine = lax.all_to_all(spread, ("col", "sub"), split_axis=0, concat_axis=1, tiled=True)
    own = lax.all_gather(basis_vectors, ("col", "sub"), axis=1, tiled=True)
    part = lax.dot_general(
        matrix,
        own,
        (((0,), (0,)), ((), ())),
        precision=lax.Precision.HIGH,
        preferred_element_type=jnp.float32,
    )
    part = part.reshape(per, R, piece, K).transpose(1, 0, 2, 3).reshape(R * per * piece, K)
    image = lax.psum_scatter(part, "row", scatter_dimension=0, tiled=True)
    partial_proj = lax.dot_general(
        mine,
        image,
        (((0,), (0,)), ((), ())),
        precision=lax.Precision.HIGH,
        preferred_element_type=jnp.float32,
    )
    proj = lax.psum_scatter(partial_proj, "row", scatter_dimension=0, tiled=True)
    proj = lax.psum_scatter(proj, ("col", "sub"), scatter_dimension=1, tiled=True)
    child_block = lax.all_gather(proj, "sub", axis=1, tiled=True)
    row_ids = (
        jnp.arange(child_block.shape[0], dtype=jnp.int32)
        + lax.axis_index("row") * child_block.shape[0]
    )
    col_ids = (
        jnp.arange(child_block.shape[1], dtype=jnp.int32)
        + lax.axis_index("col") * child_block.shape[1]
    )
    leading = split_size[0]
    row_first = row_ids < leading
    col_first = col_ids < leading
    mask_one = row_first[:, None] & col_first[None, :]
    mask_two = jnp.logical_not(row_first)[:, None] & jnp.logical_not(col_first)[None, :]
    selected = jnp.where(lax.axis_index("sub") == 0, mask_one, mask_two)
    return jnp.where(selected, child_block, jnp.zeros((), jnp.float32))[None]


def solution(mesh):
    placed = (
        P(("groups", "row"), ("col", "sub")),
        P(("groups", "row"), ("col", "sub")),
        P("groups"),
    )
    return jax.shard_map(
        shards,
        mesh=mesh,
        in_specs=placed,
        out_specs=P("sub", ("groups", "row"), "col"),
        check_vma=False,
    )
```

profile of v0, /device:TPU:0, one launch (start us, length us, event | category | flops | bytes accessed | tf_op | source)
XLA Modules:
  0.0 417.1 jit_solution(6435462178155145965)
XLA Ops:
  6.5 0.0 all-gather.2.cloned.1.call-start
  6.5 0.7 all-gather.2.cloned.1.call-update
  7.3 0.0 reduce-scatter.4.cloned.1.call-start
  7.3 62.6 %all-gather.2.cloned.1.call-done = f32[2048,1024]{1,0:T(8,128)} async-done(((f32[2048,256]{1,0:T(8,128)}), f32[2048,1024]{1,0:T(8,128)}) %all-gather.2.cloned.1.call-update) | async-done | bytes 8388624 | tf_op jit(solution)/shard_map/all_gather | solution.py:18
  69.9 33.4 %fusion.2 = f32[2048,1024]{1,0:T(8,128)} fusion(f32[2048,2048]{1,0:T(8,128)} %param.3, f32[2048,1024]{1,0:T(8,128)} %all-gather.2.cloned.1.call-done), kind=kOutput, calls=%fused_computation.6 | convolution fusion | flops 25769803776 | bytes 33554432 | tf_op jit(solution)/shard_map/dot_general | solution.py:19
  103.3 0.0 copy-start
  103.3 0.0 reduce-scatter.4.cloned.1.call-update
  103.4 0.0 reduce-scatter.6.cloned.1.call-start
  103.4 1.5 copy-done
  104.9 109.4 %all_to_all.25 = f32[4,512,256]{2,1,0:T(8,128)S(1)} all-to-all(f32[4,512,256]{2,1,0:T(8,128)S(1)} %bitcast.14), channel_id=1, replica_groups=mesh['groups'=2,'row'=4,'col'=2,'sub'=2] {'row'}, dimensions={0} | all-to-all | bytes 4194304 | tf_op jit(solution)/shard_map/all_to_all | solution.py:16
  214.3 28.1 %all_to_all.26 = f32[4,512,256]{2,1,0:T(8,128)S(1)} all-to-all(f32[4,512,256]{2,1,0:T(8,128)S(1)} %all_to_all.25), channel_id=1, replica_groups=mesh['groups'=2,'row'=4,'col'=2,'sub'=2] {'col','sub'}, dimensions={0} | all-to-all | bytes 4194304 | tf_op jit(solution)/shard_map/all_to_all | solution.py:17
  242.4 1.8 copy.6
  244.3 42.5 %reduce-scatter.4.cloned.1.call-done = f32[512,1024]{1,0:T(8,128)} async-done(((f32[2048,1024]{1,0:T(8,128)}), f32[512,1024]{1,0:T(8,128)}) %reduce-scatter.4.cloned.1.call-update) | async-done | bytes 2097168 | tf_op jit(solution)/shard_map/reduce_scatter | solution.py:27
  286.8 10.8 %convolution_bitcast_fusion = f32[1024,1024]{0,1:T(8,128)} fusion(f32[512,1024]{1,0:T(8,128)} %reduce-scatter.4.cloned.1.call-done, f32[512,1024]{0,1:T(8,128)} %bitcast.16), kind=kOutput, calls=%fused_computation | convolution fusion | flops 3221225472 | bytes 8388608 | tf_op jit(solution)/shard_map/dot_general | solution.py:28
  297.6 0.0 reduce-scatter.6.cloned.1.call-update
  297.6 0.0 reduce-scatter.8.cloned.1.call-start
  297.7 81.6 %reduce-scatter.6.cloned.1.call-done = f32[256,1024]{0,1:T(8,128)} async-done(((f32[1024,1024]{0,1:T(8,128)}), f32[256,1024]{0,1:T(8,128)}) %reduce-scatter.6.cloned.1.call-update) | async-done | bytes 1048592 | tf_op jit(solution)/shard_map/reduce_scatter | solution.py:35
  379.3 0.0 reduce-scatter.8.cloned.1.call-update
  380.0 27.0 %reduce-scatter.8.cloned.1.call-done = f32[256,256]{0,1:T(8,128)} async-done(((f32[256,1024]{0,1:T(8,128)}), f32[256,256]{0,1:T(8,128)}) %reduce-scatter.8.cloned.1.call-update) | async-done | bytes 262160 | tf_op jit(solution)/shard_map/reduce_scatter | solution.py:36
  407.0 2.4 all_gather.7
  409.4 0.2 select_bitcast_fusion
  409.6 1.0 copy.7
  (2 shorter events, 0.0 us)
Async XLA Ops:
  6.5 63.4 %all-gather.2.cloned.1.call-start = ((), (), s32[]{:S(2)}) async-start(), calls=%async_computation.5 | async-start | bytes 10485760 | tf_op jit(solution)/shard_map/all_gather | solution.py:18
  7.3 279.5 %reduce-scatter.4.cloned.1.call-start = ((), (), s32[]{:S(2)}) async-start(), calls=%async_computation.6 | async-start | bytes 10485760 | tf_op jit(solution)/shard_map/reduce_scatter | solution.py:27
  103.3 1.6 copy-start
  103.4 275.9 %reduce-scatter.6.cloned.1.call-start = ((), (), s32[]{:S(2)}) async-start(), calls=%async_computation.7 | async-start | bytes 5242880 | tf_op jit(solution)/shard_map/reduce_scatter | solution.py:35
  297.6 109.3 %reduce-scatter.8.cloned.1.call-start = ((), (), s32[]{:S(2)}) async-start(), calls=%async_computation.8 | async-start | bytes 1310720 | tf_op jit(solution)/shard_map/reduce_scatter | solution.py:36
Sparse Core Ops, SparseCore 0:
  8.9 60.9 all-gather.1
  103.5 183.2 reduce-scatter.3
  297.8 81.4 reduce-scatter.5
  381.7 25.2 reduce-scatter.7
where the time goes:
time: 417 us
  waiting for transfers between devices  214 us (51%)
  blocking collectives  140 us (34%)
  matrix products  44.3 us (11%)
  between operations  13.8 us (3%)
  local copies, waits for them, and re-layouts  4.35 us (1%)
    all_to_all x1, blocking collectives, shards(): lax.all_to_all(basis_vectors, 'row', split_axis=0, concat_axis=0, tiled=T...  109 us
    reduce_scatter x1, waiting for transfers between devices, shards(): lax.psum_scatter(partial_proj, 'row', scatter_dimension=0, tiled=True)  81.6 us
    all_gather x1, waiting for transfers between devices, shards(): own = lax.all_gather(basis_vectors, ('col', 'sub'), axis=1, tiled=True)  62.6 us
    reduce_scatter x1, waiting for transfers between devices, shards(): image = lax.psum_scatter(part, 'row', scatter_dimension=0, tiled=True)  42.5 us
    dot_general x1, matrix products, shards(): lax.dot_general(matrix, own, (((0,), (0,)), ((), ())), precision=lax.Prec...  33.4 us
    all_to_all x1, blocking collectives, shards(): lax.all_to_all(spread, ('col', 'sub'), split_axis=0, concat_axis=1, tiled...  28.1 us
    reduce_scatter x1, waiting for transfers between devices, shards(): lax.psum_scatter(proj, ('col', 'sub'), scatter_dimension=1, tiled=True)  27 us
    dot_general x1, matrix products, shards(): lax.dot_general(mine, image, (((0,), (0,)), ((), ())), precision=lax.Prec...  10.8 us
  transfers between devices with their start and end apart: 4, of which 4 were waited for; matrix products, arithmetic and copies ran while one was open for 0% of the time, Pallas kernels for 0%

commit v1 on v0

--- a/solution.py
+++ b/solution.py
@@ -15,7 +15,15 @@
     piece = m // R
     spread = lax.all_to_all(basis_vectors, "row", split_axis=0, concat_axis=0, tiled=True)
     mine = lax.all_to_all(spread, ("col", "sub"), split_axis=0, concat_axis=1, tiled=True)
-    own = lax.all_gather(basis_vectors, ("col", "sub"), axis=1, tiled=True)
+    own = jnp.concatenate(
+        lax.all_to_all(
+            jnp.stack([basis_vectors for _ in range(lax.axis_size(("col", "sub")))]),
+            ("col", "sub"),
+            0,
+            0,
+        ),
+        axis=1,
+    )
     part = lax.dot_general(
         matrix,
         own,

time: 417 us -> 479 us (1.15)
  blocking collectives: 140 us -> 237 us
  waiting for transfers between devices: 214 us -> 151 us
  matrix products: 44.3 us -> 69 us
    all_to_all x0 -> x1, blocking collectives: none -> 97.1 us  [shards(): lax.all_to_all(jnp.stack([basis_vectors for _ in range(lax.axis_size(('co...]
    all_gather x1 -> x0, waiting for transfers between devices: 62.6 us -> none  [shards(): own = lax.all_gather(basis_vectors, ('col', 'sub'), axis=1, tiled=True)]
    dot_general x1, matrix products: 33.4 us -> 58.2 us  [shards(): lax.dot_general(matrix, own, (((0,), (0,)), ((), ())), precision=lax.Prec...]
  transfers between devices with their start and end apart: 4 -> 3, of which waited for: 4 -> 3; matrix products, arithmetic and copies ran while one was open for 0% -> 0% of each run, Pallas kernels for 0% -> 0%
where the time goes in v1:
time: 479 us
  blocking collectives  237 us (49%)
  waiting for transfers between devices  151 us (32%)
  matrix products  69 us (14%)
  between operations  13.8 us (3%)
  local copies, waits for them, and re-layouts  7.28 us (2%)
    all_to_all x1, blocking collectives, shards(): lax.all_to_all(basis_vectors, 'row', split_axis=0, concat_axis=0, tiled=T...  109 us
    all_to_all x1, blocking collectives, shards(): lax.all_to_all(jnp.stack([basis_vectors for _ in range(lax.axis_size(('co...  97.1 us
    reduce_scatter x1, waiting for transfers between devices, shards(): lax.psum_scatter(partial_proj, 'row', scatter_dimension=0, tiled=True)  80.9 us
    dot_general x1, matrix products, shards(): lax.dot_general(matrix, own, (((0,), (0,)), ((), ())), precision=lax.Prec...  58.2 us
    reduce_scatter x1, waiting for transfers between devices, shards(): image = lax.psum_scatter(part, 'row', scatter_dimension=0, tiled=True)  43.1 us
    all_to_all x1, blocking collectives, shards(): lax.all_to_all(spread, ('col', 'sub'), split_axis=0, concat_axis=1, tiled...  28.1 us
    reduce_scatter x1, waiting for transfers between devices, shards(): lax.psum_scatter(proj, ('col', 'sub'), scatter_dimension=1, tiled=True)  27.1 us
    dot_general x1, matrix products, shards(): lax.dot_general(mine, image, (((0,), (0,)), ((), ())), precision=lax.Prec...  10.8 us
  transfers between devices with their start and end apart: 3, of which 3 were waited for; matrix products, arithmetic and copies ran while one was open for 0% of the time, Pallas kernels for 0%

profile of v1, /device:TPU:0, one launch (start us, length us, event | category | flops | bytes accessed | tf_op | source)
XLA Modules:
  0.0 478.6 jit_solution(4890574343754657248)
XLA Ops:
  6.5 0.0 reduce-scatter.4.cloned.1.call-start
  6.5 1.9 copy.7
  8.5 1.0 stack.2
  9.5 97.1 %all_to_all.30 = f32[4,2048,256]{1,2,0:T(8,128)S(1)} all-to-all(f32[4,2048,256]{1,2,0:T(8,128)S(1)} %stack.2), channel_id=1, replica_groups=mesh['groups'=2,'row'=4,'col'=2,'sub'=2] {'col','sub'}, dimensions={0} | all-to-all | bytes 16777216 | tf_op jit(solution)/shard_map/all_to_all | solution.py:19
  106.6 58.2 %fusion.2 = f32[2048,1024]{1,0:T(8,128)} fusion(f32[2048,2048]{1,0:T(8,128)} %param.3, f32[2048,1024]{0,1:T(8,128)S(1)} %bitcast.17), kind=kOutput, calls=%fused_computation.6 | convolution fusion | flops 25769803776 | bytes 33554432 | tf_op jit(solution)/shard_map/dot_general | solution.py:27
  164.8 0.0 copy-start
  164.8 0.0 reduce-scatter.4.cloned.1.call-update
  164.8 0.0 reduce-scatter.6.cloned.1.call-start
  164.9 1.5 copy-done
  166.4 109.4 %all_to_all.31 = f32[4,512,256]{2,1,0:T(8,128)S(1)} all-to-all(f32[4,512,256]{2,1,0:T(8,128)S(1)} %bitcast.18), channel_id=1, replica_groups=mesh['groups'=2,'row'=4,'col'=2,'sub'=2] {'row'}, dimensions={0} | all-to-all | bytes 4194304 | tf_op jit(solution)/shard_map/all_to_all | solution.py:16
  275.8 28.1 %all_to_all.32 = f32[4,512,256]{2,1,0:T(8,128)S(1)} all-to-all(f32[4,512,256]{2,1,0:T(8,128)S(1)} %all_to_all.31), channel_id=1, replica_groups=mesh['groups'=2,'row'=4,'col'=2,'sub'=2] {'col','sub'}, dimensions={0} | all-to-all | bytes 4194304 | tf_op jit(solution)/shard_map/all_to_all | solution.py:17
  303.9 1.8 copy.8
  305.8 43.1 %reduce-scatter.4.cloned.1.call-done = f32[512,1024]{1,0:T(8,128)} async-done(((f32[2048,1024]{1,0:T(8,128)}), f32[512,1024]{1,0:T(8,128)}) %reduce-scatter.4.cloned.1.call-update) | async-done | bytes 2097168 | tf_op jit(solution)/shard_map/reduce_scatter | solution.py:35
  348.8 10.8 %convolution_bitcast_fusion = f32[1024,1024]{0,1:T(8,128)} fusion(f32[512,1024]{1,0:T(8,128)} %reduce-scatter.4.cloned.1.call-done, f32[512,1024]{0,1:T(8,128)} %bitcast.20), kind=kOutput, calls=%fused_computation | convolution fusion | flops 3221225472 | bytes 8388608 | tf_op jit(solution)/shard_map/dot_general | solution.py:36
  359.7 0.0 reduce-scatter.6.cloned.1.call-update
  359.7 0.0 reduce-scatter.8.cloned.1.call-start
  359.7 80.9 %reduce-scatter.6.cloned.1.call-done = f32[256,1024]{0,1:T(8,128)} async-done(((f32[1024,1024]{0,1:T(8,128)}), f32[256,1024]{0,1:T(8,128)}) %reduce-scatter.6.cloned.1.call-update) | async-done | bytes 1048592 | tf_op jit(solution)/shard_map/reduce_scatter | solution.py:43
  440.6 0.0 reduce-scatter.8.cloned.1.call-update
  441.4 27.1 %reduce-scatter.8.cloned.1.call-done = f32[256,256]{0,1:T(8,128)} async-done(((f32[256,1024]{0,1:T(8,128)}), f32[256,256]{0,1:T(8,128)}) %reduce-scatter.8.cloned.1.call-update) | async-done | bytes 262160 | tf_op jit(solution)/shard_map/reduce_scatter | solution.py:44
  468.5 2.4 all_gather.3
  470.9 0.2 select_bitcast_fusion
  471.1 1.0 copy.9
  (2 shorter events, 0.0 us)
Async XLA Ops:
  6.5 342.3 %reduce-scatter.4.cloned.1.call-start = ((), (), s32[]{:S(2)}) async-start(), calls=%async_computation.6 | async-start | bytes 10485760 | tf_op jit(solution)/shard_map/reduce_scatter | solution.py:35
  164.8 1.6 copy-start
  164.8 275.8 %reduce-scatter.6.cloned.1.call-start = ((), (), s32[]{:S(2)}) async-start(), calls=%async_computation.7 | async-start | bytes 5242880 | tf_op jit(solution)/shard_map/reduce_scatter | solution.py:43
  359.7 108.8 %reduce-scatter.8.cloned.1.call-start = ((), (), s32[]{:S(2)}) async-start(), calls=%async_computation.8 | async-start | bytes 1310720 | tf_op jit(solution)/shard_map/reduce_scatter | solution.py:44
Sparse Core Ops, SparseCore 0:
  164.9 183.8 reduce-scatter.3
  359.8 80.7 reduce-scatter.5
  443.2 25.2 reduce-scatter.7
